TPU v7x, 32 devices: a whole 2x2x4 slice. The times are simulated.
32 devices in a mesh: slab: 4 (over z), swap: 8 (over y, x, core).
Axes of the slice: x: 2, y: 2, z: 4, core: 2. Of those that a mesh axis runs over, the one named last changes fastest.
Arguments:
- fluid_state: float32 [2, 128, 128, 256], P(None, ('slab', 'swap')), may hold values from -0.45 to 1.6, as said below
- material: int32 [128, 128, 256], P(('slab', 'swap')), may hold values from 0 to 7
- table_colour: float32 [3, 8], replicated, may hold values from 0.2 to 2
- table_extinction: float32 [8], replicated, may hold values from 0.2 to 1.5
Outputs:
- new_density: float32 [128, 128, 256], P(('slab', 'swap'))
- rendered: float32 [4, 32768], P(None, 'swap')
Inputs may be any that keep to these rules, and one draw needn't show every extreme that they name: fluid_state[0] is the density, between 0.6 and 1.6; fluid_state[1] is the momentum along the view axis, between -0.45 and 0.45.
All inputs are finite; a program needn't handle non-finite values.
Results may differ from a plain program's by a relative error of at most 0.0003.
Values sent between devices are 32-bit elements; how exact they have to be, the bound alone decides.
A program may use at most 64 MiB of HBM per device.

v0:
```python
import functools

import jax
import jax.numpy as jnp
from jax import lax
from jax.experimental import pallas as pl
from jax.experimental.pallas import tpu as pltpu
from jax.sharding import PartitionSpec as P

COURANT = 0.4
DEPTH_SCALE = 2.5
STEPS = 4
VMEM_BYTES = 67043328
SPARE = 128 * 1024
MESH = pl.DeviceIdType.MESH


def largest_divisor(number, limit):
    return max(d for d in range(1, limit + 1) if number % d == 0)


def advance(state, density, momentum):
    old_density, old_momentum, old_flux, old_speed, old_face_d, old_face_m = state
    velocity = momentum / density
    speed = jnp.abs(velocity) + 1.0
    flux = momentum * velocity + density
    face_speed = jnp.maximum(old_speed, speed)
    face_d = (old_momentum + momentum) - face_speed * (density - old_density)
    face_m = (old_flux + flux) - face_speed * (momentum - old_momentum)
    half = 0.5 * COURANT
    new_density = old_density - half * (face_d - old_face_d)
    new_momentum = old_momentum - half * (face_m - old_face_m)
    return (density, momentum, flux, speed, face_d, face_m), new_density, new_momentum


def lookup(masks, values):
    for mask in masks:
        values = [
            jnp.where(mask, values[i + 1], values[i]) if i + 1 < len(values) else values[i]
            for i in range(0, len(values), 2)
        ]
    return values[0]


def kernel(
    dims,
    fields,
    material,
    colour_table,
    extinction_table,
    out_density,
    out_image,
    staged,
    staged_material,
    held,
    held_material,
    new_density,
    pieces,
    image,
    image_sem,
    stage_sem,
    send_sem,
    field_sem,
    halo_sem,
    material_sem,
    back_sem,
    piece_sem,
):
    slabs, members, depth, rows, cols, chunk_rows, chunk_cols = dims
    slab = lax.axis_index("slab")
    me = lax.axis_index("swap")
    layers = members * depth
    width = STEPS
    across = cols // chunk_cols
    chunks = (rows // chunk_rows) * across
    materials = extinction_table.shape[0]

    def spot(c):
        return (
            pl.ds(c // across * chunk_rows, chunk_rows),
            pl.ds(c % across * chunk_cols, chunk_cols),
        )

    loads = (
        pltpu.make_async_copy(fields, staged, stage_sem.at[0]),
        pltpu.make_async_copy(material, staged_material, stage_sem.at[1]),
    )
    for load in loads:
        load.start()

    barrier = pltpu.get_barrier_semaphore()

    @pl.loop(1, slabs)
    def _(k):
        pl.semaphore_signal(
            barrier, inc=1, device_id=(lax.rem(slab + k, slabs), me), device_id_type=MESH
        )

    @pl.loop(1, members)
    def _(k):
        pl.semaphore_signal(
            barrier, inc=1, device_id=(slab, lax.rem(me + k, members)), device_id_type=MESH
        )

    mine = pl.ds(width + me * depth, depth)
    mine_material = pl.ds(me * depth, depth)
    pl.semaphore_wait(barrier, members - 1 + slabs - 1)

    loads[0].wait()

    def send_fields(c):
        r, l = spot(c)

        @pl.loop(1, members)
        def _(k):
            peer = lax.rem(me + k, members)
            pltpu.make_async_remote_copy(
                src_ref=staged.at[:, :, peer, r, l],
                dst_ref=held.at[c, :, mine],
                send_sem=send_sem.at[0],
                recv_sem=field_sem.at[c, me],
                device_id=(slab, peer),
                device_id_type=MESH,
            ).start()

    def send_material(c):
        r, l = spot(c)

        @pl.loop(1, members)
        def _(k):
            peer = lax.rem(me + k, members)
            pltpu.make_async_remote_copy(
                src_ref=staged_material.at[:, peer, r, l],
                dst_ref=held_material.at[c, mine_material],
                send_sem=send_sem.at[1],
                recv_sem=material_sem.at[c],
                device_id=(slab, peer),
                device_id_type=MESH,
            ).start()

    send_fields(0)
    loads[1].wait()
    for c in range(chunks):
        if c + 1 < chunks:
            send_fields(c + 1)
        send_material(c)

    for c in range(chunks):
        r, l = spot(c)
        pltpu.make_async_copy(
            staged.at[:, :, me, r, l], held.at[c, :, mine], field_sem.at[c, me]
        ).start()
        pltpu.make_async_copy(
            staged_material.at[:, me, r, l], held_material.at[c, mine_material], material_sem.at[c]
        ).start()

    def wait_for(ref, sem):
        pltpu.make_async_copy(ref, ref, sem).wait()

    def pass_halos(c):
        for side, (owner, start, target, to) in enumerate((
            (members - 1, layers, 0, lax.rem(slab + 1, slabs)),
            (0, width, width + layers, lax.rem(slab + slabs - 1, slabs)),
        )):
            wait_for(held.at[c, :, pl.ds(width + owner * depth, depth)], field_sem.at[c, owner])
            pltpu.make_async_remote_copy(
                src_ref=held.at[c, :, pl.ds(start, width)],
                dst_ref=held.at[c, :, pl.ds(target, width)],
                send_sem=send_sem.at[2],
                recv_sem=halo_sem.at[c, side],
                device_id=(to, me),
                device_id_type=MESH,
            ).start()

    total = layers + 2 * width
    unroll = largest_divisor(total, 40)

    def sweep(c):
        one = jnp.ones((chunk_rows, chunk_cols), jnp.float32)

        def block(b, states):
            for u in range(unroll):
                i = b * unroll + u
                density, momentum = held[c, 0, i], held[c, 1, i]
                following = []
                for state in states:
                    state, density, momentum = advance(state, density, momentum)
                    following.append(state)
                states = tuple(following)
                new_density[c, i] = density
            return states

        lax.fori_loop(0, total // unroll, block, ((one,) * 6,) * STEPS)

    scale = DEPTH_SCALE / (slabs * layers)
    step = largest_divisor(layers, 16)

    def render(c):
        wait_for(held_material.at[c], material_sem.at[c])
        zero = jnp.zeros((chunk_rows, chunk_cols), jnp.float32)
        rates = [extinction_table[n] * (-scale) for n in range(materials)]
        colours = [[colour_table[ch, n] for n in range(materials)] for ch in range(3)]

        def block(b, carry):
            through, sums = carry
            for u in range(step):
                i = b * step + u
                row = held_material[c, i]
                masks = [(row & (1 << bit)) != 0 for bit in range((materials - 1).bit_length())]
                rate = lookup(masks, rates)
                kept = jnp.exp(rate * new_density[c, 2 * width + i])
                weight = through * (1.0 - kept)
                sums = tuple(s + weight * lookup(masks, t) for s, t in zip(sums, colours))
                through = through * kept
            return through, sums

        through, sums = lax.fori_loop(0, layers // step, block, (zero + 1.0, (zero,) * 3))
        for ch in range(3):
            pieces[c, slab, ch] = sums[ch]
        pieces[c, slab, 3] = through

        @pl.loop(1, slabs)
        def _(k):
            pltpu.make_async_remote_copy(
                src_ref=pieces.at[c, slab],
                dst_ref=pieces.at[c, slab],
                send_sem=send_sem.at[4],
                recv_sem=piece_sem.at[c],
                device_id=(lax.rem(slab + k, slabs), me),
                device_id_type=MESH,
            ).start()

    pass_halos(0)

    @pl.loop(0, chunks)
    def _(c):
        @pl.when(c + 1 < chunks)
        def _():
            pass_halos(c + 1)

        @pl.loop(1, members - 1)
        def _(m):
            wait_for(held.at[c, :, pl.ds(width + m * depth, depth)], field_sem.at[c, m])

        for side in range(2):
            wait_for(held.at[c, :, pl.ds(0, width)], halo_sem.at[c, side])
        sweep(c)
        r = pl.ds(pl.multiple_of(c // across * chunk_rows, chunk_rows), chunk_rows)
        l = pl.ds(pl.multiple_of(c % across * chunk_cols, chunk_cols), chunk_cols)

        @pl.loop(1, members)
        def _(k):
            peer = lax.rem(me + k, members)
            pltpu.make_async_remote_copy(
                src_ref=new_density.at[c, pl.ds(2 * width + peer * depth, depth)],
                dst_ref=out_density.at[:, me, r, l],
                send_sem=send_sem.at[3],
                recv_sem=back_sem,
                device_id=(slab, peer),
                device_id_type=MESH,
            ).start()

        pltpu.make_async_copy(
            new_density.at[c, pl.ds(2 * width + me * depth, depth)],
            out_density.at[:, me, r, l],
            back_sem,
        ).start()

        @pl.when(c > 0)
        def _():
            render(c - 1)

    render(chunks - 1)

    for c in range(chunks):
        wait_for(pieces.at[c, pl.ds(0, slabs - 1)], piece_sem.at[c])
        through = pieces[c, 0, 3]
        sums = [pieces[c, 0, ch] for ch in range(3)]
        for s in range(1, slabs):
            sums = [total_ch + through * pieces[c, s, ch] for ch, total_ch in enumerate(sums)]
            through = through * pieces[c, s, 3]
        for ch, value in enumerate(sums + [1.0 - through]):
            for q in range(chunk_rows):
                start = (c // across * chunk_rows + q) * cols + c % across * chunk_cols
                image[ch : ch + 1, start : start + chunk_cols] = value[q : q + 1]
    image_copy = pltpu.make_async_copy(image, out_image, image_sem)
    image_copy.start()

    others = pl.ds(0, members - 1)
    wait_for(staged.at[:, :, others], send_sem.at[0])
    wait_for(staged_material.at[:, others], send_sem.at[1])
    wait_for(held.at[:, :, pl.ds(0, 2 * width)], send_sem.at[2])
    wait_for(new_density.at[:, pl.ds(0, (members - 1) * depth)], send_sem.at[3])
    wait_for(pieces.at[:, pl.ds(0, slabs - 1)], send_sem.at[4])
    wait_for(out_density, back_sem)
    image_copy.wait()


def put_kernel(density, image, out_density, out_image, sems):
    copies = (
        pltpu.make_async_copy(density, out_density, sems.at[0]),
        pltpu.make_async_copy(image, out_image, sems.at[1]),
    )
    for copy in copies:
        copy.start()
    for copy in copies:
        copy.wait()


def write_out(density, image):
    return pl.pallas_call(
        put_kernel,
        out_shape=(
            jax.ShapeDtypeStruct(density.shape, density.dtype),
            jax.ShapeDtypeStruct(image.shape, image.dtype),
        ),
        in_specs=[pl.BlockSpec(memory_space=pl.ANY)] * 2,
        out_specs=(pl.BlockSpec(memory_space=pl.ANY),) * 2,
        scratch_shapes=[pltpu.SemaphoreType.DMA((2,))],
        compiler_params=pltpu.CompilerParams(vmem_limit_bytes=1024 * 1024),
    )(density, image)


def per_device(fluid_state, material, table_colour, table_extinction):
    slabs = lax.axis_size("slab")
    members = lax.axis_size("swap")
    _, depth, height, cols = fluid_state.shape
    rows = height // members
    chunk_rows = 8 if rows % 8 == 0 else rows
    chunk_cols = cols
    chunks = (rows // chunk_rows) * (cols // chunk_cols)
    layers = members * depth
    tile = (chunk_rows, chunk_cols)
    grant = VMEM_BYTES - 4 * rows * cols * (depth * members + 4) - SPARE
    dims = (slabs, members, depth, rows, cols, chunk_rows, chunk_cols)
    density, image = pl.pallas_call(
        functools.partial(kernel, dims),
        out_shape=(
            pltpu.VMEM((depth, members, rows, cols), jnp.float32),
            pltpu.VMEM((4, rows * cols), jnp.float32),
        ),
        in_specs=[
            pl.BlockSpec(memory_space=pltpu.HBM),
            pl.BlockSpec(memory_space=pltpu.HBM),
            pl.BlockSpec(memory_space=pltpu.SMEM),
            pl.BlockSpec(memory_space=pltpu.SMEM),
        ],
        out_specs=(
            pl.BlockSpec(memory_space=pl.ANY),
            pl.BlockSpec(memory_space=pl.ANY),
        ),
        scratch_shapes=[
            pltpu.VMEM((2, depth, members, rows, cols), jnp.float32),
            pltpu.VMEM((depth, members, rows, cols), jnp.int32),
            pltpu.VMEM((chunks, 2, layers + 2 * STEPS) + tile, jnp.float32),
            pltpu.VMEM((chunks, layers) + tile, jnp.int32),
            pltpu.VMEM((chunks, layers + 2 * STEPS) + tile, jnp.float32),
            pltpu.VMEM((chunks, slabs, 4) + tile, jnp.float32),
            pltpu.VMEM((4, rows * cols), jnp.float32),
            pltpu.SemaphoreType.DMA,
            pltpu.SemaphoreType.DMA((2,)),
            pltpu.SemaphoreType.DMA((5,)),
            pltpu.SemaphoreType.DMA((chunks, members)),
            pltpu.SemaphoreType.DMA((chunks, 2)),
            pltpu.SemaphoreType.DMA((chunks,)),
            pltpu.SemaphoreType.DMA,
            pltpu.SemaphoreType.DMA((chunks,)),
        ],
        compiler_params=pltpu.CompilerParams(
            collective_id=0, has_side_effects=True, vmem_limit_bytes=grant
        ),
    )(
        fluid_state.reshape(2, depth, members, rows, cols),
        material.reshape(depth, members, rows, cols),
        table_colour,
        table_extinction,
    )
    return write_out(density.reshape(depth, height, cols), image)


def solution(mesh):
    return jax.shard_map(
        per_device,
        mesh=mesh,
        in_specs=(P(None, ("slab", "swap"), None, None), P(("slab", "swap"), None, None), P(), P()),
        out_specs=(P(("slab", "swap"), None, None), P(None, "swap")),
        check_vma=False,
    )
```

profile of v0, /device:TPU:0, one launch (start us, length us, event | category | flops | bytes accessed | tf_op | source)
XLA Modules:
  0.0 31.9 jit_solution(16797103292062739929)
XLA Ops:
  0.6 30.4 %shard_map.59 = (f32[4,8,16,256]{3,2,1,0:T(8,128)S(1)}, f32[4,4096]{1,0:T(4,128)S(1)}) custom-call(f32[2,4,8,16,256]{4,3,2,1,0:T(8,128)} %bitcast.4, s32[4,8,16,256]{3,2,1,0:T(8,128)} %bitcast.5, f32[3,8]{1,0:T(4,128)} %colour_table.1, f32[8]{0:T(128)} %extinction_table.1), custom_call_target="tpu_custom_call" | custom-call | tf_op jit(solution)/shard_map/pallas_call | solution.py:336
  31.0 0.8 %shard_map.60 = (f32[4,128,256]{2,1,0:T(8,128)}, f32[4,4096]{1,0:T(4,128)}) custom-call(f32[4,128,256]{2,1,0:T(8,128)S(1)} %bitcast.3, f32[4,4096]{1,0:T(4,128)S(1)} %get-tuple-element.5.image), custom_call_target="tpu_custom_call" | custom-call | tf_op jit(solution)/shard_map/pallas_call | solution.py:311
where the time goes:
time: 32 us; the launch traced here: 31.9 us
  Pallas kernels  31.2 us (98%)
  between operations  0.64 us (2%)
    pallas_call x1, Pallas kernels, per_device(): pl.pallas_call(functools.partial(kernel, dims), out_shape=(pltpu.VMEM((de...  30.4 us
    pallas_call x1, Pallas kernels, write_out(): pl.pallas_call(put_kernel, out_shape=(jax.ShapeDtypeStruct(density.shape,...  0.82 us

commit v1 on v0

v1 whole, which is shorter than its diff:
```python
import functools

import jax
import jax.numpy as jnp
from jax import lax
from jax.experimental import pallas as pl
from jax.experimental.pallas import tpu as pltpu
from jax.sharding import PartitionSpec as P

COURANT = 0.4
DEPTH_SCALE = 2.5
STEPS = 4
VMEM_BYTES = 67043328
SPARE = 128 * 1024
MESH = pl.DeviceIdType.MESH


def largest_divisor(number, limit):
    return max(d for d in range(1, limit + 1) if number % d == 0)


def advance(state, density, momentum):
    velocity = momentum / density
    speed = jnp.abs(velocity) + 1.0
    flux = momentum * velocity + density
    if state is None:
        return (density, momentum, flux, speed, None, None), None
    old_density, old_momentum, old_flux, old_speed, old_face_d, old_face_m = state
    face_speed = jnp.maximum(old_speed, speed)
    face_d = (old_momentum + momentum) - face_speed * (density - old_density)
    face_m = (old_flux + flux) - face_speed * (momentum - old_momentum)
    state = (density, momentum, flux, speed, face_d, face_m)
    if old_face_d is None:
        return state, None
    half = 0.5 * COURANT
    new_density = old_density - half * (face_d - old_face_d)
    new_momentum = old_momentum - half * (face_m - old_face_m)
    return state, (new_density, new_momentum)


def lookup(masks, values):
    for mask in masks:
        values = [
            jnp.where(mask, values[i + 1], values[i]) if i + 1 < len(values) else values[i]
            for i in range(0, len(values), 2)
        ]
    return values[0]


def kernel(
    dims,
    fields,
    material,
    colour_source,
    extinction_source,
    out_density,
    out_image,
    staged,
    staged_material,
    held,
    held_material,
    new_density,
    pieces,
    image,
    colour_table,
    extinction_table,
    table_sem,
    image_sem,
    load_sem,
    load_material_sem,
    send_sem,
    field_sem,
    halo_sem,
    material_sem,
    back_sem,
    piece_sem,
    plane_sem,
    ready_sem,
    go_sem,
):
    slabs, members, depth, rows, cols, chunk_rows, chunk_cols = dims
    slab = lax.axis_index("slab")
    me = lax.axis_index("swap")
    gate = 1
    layers = members * depth
    width = STEPS
    across = cols // chunk_cols
    chunks = (rows // chunk_rows) * across
    materials = extinction_table.shape[0]

    def spot(c):
        return (
            pl.ds(pl.multiple_of(c // across * chunk_rows, chunk_rows), chunk_rows),
            pl.ds(pl.multiple_of(c % across * chunk_cols, chunk_cols), chunk_cols),
        )

    loads = []
    material_loads = []
    mine = pl.ds(width + me * depth, depth)
    mine_material = pl.ds(me * depth, depth)
    for c in range(chunks):
        r, l = spot(c)
        loads.append(
            pltpu.make_async_copy(
                fields.at[:, :, :, r, l], staged.at[:, :, :, r, l], load_sem.at[c]
            )
        )
        loads[-1].start()
    for c in range(chunks):
        r, l = spot(c)
        material_loads.append(
            pltpu.make_async_copy(
                material.at[:, :, r, l],
                staged_material.at[:, :, r, l],
                load_material_sem.at[c],
            )
        )
        material_loads[-1].start()

    tables = (
        pltpu.make_async_copy(colour_source, colour_table, table_sem.at[0]),
        pltpu.make_async_copy(extinction_source, extinction_table, table_sem.at[1]),
    )
    for table in tables:
        table.start()

    barrier = pltpu.get_barrier_semaphore()
    behind = lax.rem(slab + slabs - 1, slabs)
    ahead = lax.rem(slab + 1, slabs)
    def to_other_slabs(sem):
        @pl.loop(1, slabs)
        def _(k):
            pl.semaphore_signal(
                sem, inc=1, device_id=(lax.rem(slab + k, slabs), me), device_id_type=MESH
            )

    def to_plane(sem):
        @pl.loop(1, members)
        def _(k):
            other = lax.rem(me + k, members)

            @pl.when(other != gate)
            def _():
                pl.semaphore_signal(sem, inc=1, device_id=(slab, other), device_id_type=MESH)

    to_plane(barrier)

    @pl.when(me == gate)
    def _():
        to_other_slabs(barrier)

    @pl.when(me != gate)
    def _():
        pl.semaphore_wait(barrier, members - 1)
        pl.semaphore_signal(plane_sem, inc=1, device_id=(slab, gate), device_id_type=MESH)

    @pl.when(me == gate)
    def _():
        pl.semaphore_wait(plane_sem, members - 1)

    def send_fields(c):
        r, l = spot(c)
        @pl.loop(1, members)
        def _(k):
            other = lax.rem(me + k, members)
            pltpu.make_async_remote_copy(
                src_ref=staged.at[:, :, other, r, l],
                dst_ref=held.at[c, :, mine],
                send_sem=send_sem.at[0],
                recv_sem=field_sem.at[c, me],
                device_id=(slab, other),
                device_id_type=MESH,
            ).start()

    def send_material(c):
        r, l = spot(c)
        @pl.loop(1, members)
        def _(k):
            other = lax.rem(me + k, members)
            pltpu.make_async_remote_copy(
                src_ref=staged_material.at[:, other, r, l],
                dst_ref=held_material.at[c, mine_material],
                send_sem=send_sem.at[1],
                recv_sem=material_sem.at[c],
                device_id=(slab, other),
                device_id_type=MESH,
            ).start()

    for c in range(chunks):
        loads[c].wait()
        send_fields(c)
    for c in range(chunks):
        material_loads[c].wait()
        send_material(c)

    for c in range(chunks):
        r, l = spot(c)
        pltpu.make_async_copy(
            staged.at[:, :, me, r, l], held.at[c, :, mine], field_sem.at[c, me]
        ).start()
        pltpu.make_async_copy(
            staged_material.at[:, me, r, l], held_material.at[c, mine_material], material_sem.at[c]
        ).start()

    @pl.when(me == gate)
    def _():
        pl.semaphore_wait(barrier, slabs - 1)
        to_other_slabs(ready_sem)
        pl.semaphore_wait(ready_sem, slabs - 1)
        to_plane(go_sem)

    @pl.when(me != gate)
    def _():
        pl.semaphore_wait(go_sem, 1)

    def wait_for(ref, sem):
        pltpu.make_async_copy(ref, ref, sem).wait()

    def pass_halos(c):
        for side, (owner, start, target, to) in enumerate((
            (members - 1, layers, 0, ahead),
            (0, width, width + layers, behind),
        )):
            wait_for(held.at[c, :, pl.ds(width + owner * depth, depth)], field_sem.at[c, owner])
            pltpu.make_async_remote_copy(
                src_ref=held.at[c, :, pl.ds(start, width)],
                dst_ref=held.at[c, :, pl.ds(target, width)],
                send_sem=send_sem.at[2],
                recv_sem=halo_sem.at[c, side],
                device_id=(to, me),
                device_id_type=MESH,
            ).start()

    total = layers + 2 * width

    def sweep(c):
        states = [None] * STEPS
        for i in range(total):
            cell = held[c, 0, i], held[c, 1, i]
            for k in range(STEPS):
                states[k], cell = advance(states[k], *cell)
                if cell is None:
                    break
            if cell is not None:
                new_density[c, i - 2 * width] = cell[0]

    def send_back(c):
        r, l = spot(c)
        @pl.loop(1, members)
        def _(k):
            other = lax.rem(me + k, members)
            pltpu.make_async_remote_copy(
                src_ref=new_density.at[c, pl.ds(other * depth, depth)],
                dst_ref=out_density.at[:, me, r, l],
                send_sem=send_sem.at[3],
                recv_sem=back_sem,
                device_id=(slab, other),
                device_id_type=MESH,
            ).start()
        pltpu.make_async_copy(
            new_density.at[c, pl.ds(me * depth, depth)],
            out_density.at[:, me, r, l],
            back_sem,
        ).start()

    scale = DEPTH_SCALE / (slabs * layers)

    def render(c):
        wait_for(held_material.at[c], material_sem.at[c])
        zero = jnp.zeros((chunk_rows, chunk_cols), jnp.float32)
        rates = [extinction_table[n] * (-scale) for n in range(materials)]
        colours = [[colour_table[ch, n] for n in range(materials)] for ch in range(3)]

        through, sums = zero + 1.0, (zero,) * 3
        for i in range(layers):
            row = held_material[c, i]
            masks = [(row & (1 << bit)) != 0 for bit in range((materials - 1).bit_length())]
            rate = lookup(masks, rates)
            kept = jnp.exp(rate * new_density[c, i])
            weight = through * (1.0 - kept)
            sums = tuple(s + weight * lookup(masks, t) for s, t in zip(sums, colours))
            through = through * kept
        for ch in range(3):
            pieces[c, slab, ch] = sums[ch]
        pieces[c, slab, 3] = through

        @pl.loop(1, slabs)
        def _(k):
            pltpu.make_async_remote_copy(
                src_ref=pieces.at[c, slab],
                dst_ref=pieces.at[c, slab],
                send_sem=send_sem.at[4],
                recv_sem=piece_sem.at[c],
                device_id=(lax.rem(slab + k, slabs), me),
                device_id_type=MESH,
            ).start()

    pass_halos(0)
    for table in tables:
        table.wait()

    @pl.loop(0, chunks)
    def _(c):
        @pl.when(c + 1 < chunks)
        def _():
            pass_halos(c + 1)

        for m in range(1, members - 1):
            wait_for(held.at[c, :, pl.ds(width + m * depth, depth)], field_sem.at[c, m])
        for side in range(2):
            wait_for(held.at[c, :, pl.ds(0, width)], halo_sem.at[c, side])
        sweep(c)
        send_back(c)

        @pl.when(c > 0)
        def _():
            render(c - 1)

    render(chunks - 1)
    for c in range(chunks):
        wait_for(pieces.at[c, pl.ds(0, slabs - 1)], piece_sem.at[c])
        through = pieces[c, 0, 3]
        sums = [pieces[c, 0, ch] for ch in range(3)]
        for n in range(1, slabs):
            sums = [value + through * pieces[c, n, ch] for ch, value in enumerate(sums)]
            through = through * pieces[c, n, 3]
        for ch, value in enumerate(sums + [1.0 - through]):
            for q in range(chunk_rows):
                start = (c // across * chunk_rows + q) * cols + c % across * chunk_cols
                image[ch : ch + 1, start : start + chunk_cols] = value[q : q + 1]
    image_copy = pltpu.make_async_copy(image, out_image, image_sem)
    image_copy.start()

    others = pl.ds(0, members - 1)
    wait_for(staged.at[:, :, others], send_sem.at[0])
    wait_for(staged_material.at[:, others], send_sem.at[1])
    wait_for(held.at[:, :, pl.ds(0, 2 * width)], send_sem.at[2])
    wait_for(new_density.at[:, pl.ds(0, (members - 1) * depth)], send_sem.at[3])
    wait_for(pieces.at[:, pl.ds(0, slabs - 1)], send_sem.at[4])
    wait_for(out_density, back_sem)
    image_copy.wait()


def put_kernel(density, image, out_density, out_image, sems):
    copies = (
        pltpu.make_async_copy(density, out_density, sems.at[0]),
        pltpu.make_async_copy(image, out_image, sems.at[1]),
    )
    for copy in copies:
        copy.start()
    for copy in copies:
        copy.wait()


def write_out(density, image):
    return pl.pallas_call(
        put_kernel,
        out_shape=(
            jax.ShapeDtypeStruct(density.shape, density.dtype),
            jax.ShapeDtypeStruct(image.shape, image.dtype),
        ),
        in_specs=[pl.BlockSpec(memory_space=pl.ANY)] * 2,
        out_specs=(pl.BlockSpec(memory_space=pl.ANY),) * 2,
        scratch_shapes=[pltpu.SemaphoreType.DMA((2,))],
        compiler_params=pltpu.CompilerParams(vmem_limit_bytes=1024 * 1024),
    )(density, image)


def per_device(fluid_state, material, table_colour, table_extinction):
    slabs = lax.axis_size("slab")
    members = lax.axis_size("swap")
    _, depth, height, cols = fluid_state.shape
    rows = height // members
    chunk_rows = 8 if rows % 8 == 0 else rows
    chunk_cols = cols
    chunks = (rows // chunk_rows) * (cols // chunk_cols)
    layers = members * depth
    tile = (chunk_rows, chunk_cols)
    grant = VMEM_BYTES - 4 * rows * cols * (depth * members + 4) - SPARE
    dims = (slabs, members, depth, rows, cols, chunk_rows, chunk_cols)
    density, image = pl.pallas_call(
        functools.partial(kernel, dims),
        out_shape=(
            pltpu.VMEM((depth, members, rows, cols), jnp.float32),
            pltpu.VMEM((4, rows * cols), jnp.float32),
        ),
        in_specs=[
            pl.BlockSpec(memory_space=pltpu.HBM),
            pl.BlockSpec(memory_space=pltpu.HBM),
            pl.BlockSpec(memory_space=pltpu.HBM),
            pl.BlockSpec(memory_space=pltpu.HBM),
        ],
        out_specs=(
            pl.BlockSpec(memory_space=pl.ANY),
            pl.BlockSpec(memory_space=pl.ANY),
        ),
        scratch_shapes=[
            pltpu.VMEM((2, depth, members, rows, cols), jnp.float32),
            pltpu.VMEM((depth, members, rows, cols), jnp.int32),
            pltpu.VMEM((chunks, 2, layers + 2 * STEPS) + tile, jnp.float32),
            pltpu.VMEM((chunks, layers) + tile, jnp.int32),
            pltpu.VMEM((chunks, layers) + tile, jnp.float32),
            pltpu.VMEM((chunks, slabs, 4) + tile, jnp.float32),
            pltpu.VMEM((4, rows * cols), jnp.float32),
            pltpu.SMEM(table_colour.shape, jnp.float32),
            pltpu.SMEM(table_extinction.shape, jnp.float32),
            pltpu.SemaphoreType.DMA((2,)),
            pltpu.SemaphoreType.DMA,
            pltpu.SemaphoreType.DMA((chunks,)),
            pltpu.SemaphoreType.DMA((chunks,)),
            pltpu.SemaphoreType.DMA((5,)),
            pltpu.SemaphoreType.DMA((chunks, members)),
            pltpu.SemaphoreType.DMA((chunks, 2)),
            pltpu.SemaphoreType.DMA((chunks,)),
            pltpu.SemaphoreType.DMA,
            pltpu.SemaphoreType.DMA((chunks,)),
            pltpu.SemaphoreType.REGULAR,
            pltpu.SemaphoreType.REGULAR,
            pltpu.SemaphoreType.REGULAR,
        ],
        compiler_params=pltpu.CompilerParams(
            collective_id=0, has_side_effects=True, vmem_limit_bytes=grant
        ),
    )(
        fluid_state.reshape(2, depth, members, rows, cols),
        material.reshape(depth, members, rows, cols),
        table_colour,
        table_extinction,
    )
    return write_out(density.reshape(depth, height, cols), image)


def solution(mesh):
    return jax.shard_map(
        per_device,
        mesh=mesh,
        in_specs=(P(None, ("slab", "swap"), None, None), P(("slab", "swap"), None, None), P(), P()),
        out_specs=(P(("slab", "swap"), None, None), P(None, "swap")),
        check_vma=False,
    )
```

time: 32 us -> 30.7 us (0.959)
  the two profiles are of different devices: /device:TPU:0 before, /device:TPU:5 now
where the time goes in v1:
time: 30.7 us; the launch traced here: 30.2 us
  Pallas kernels  29.5 us (96%)
  between operations  0.64 us (2%)
    pallas_call x1, Pallas kernels, per_device(): pl.pallas_call(functools.partial(kernel, dims), out_shape=(pltpu.VMEM((de...  28.7 us
    pallas_call x1, Pallas kernels, write_out(): pl.pallas_call(put_kernel, out_shape=(jax.ShapeDtypeStruct(density.shape,...  0.82 us

profile of v1, /device:TPU:5, one launch (start us, length us, event | category | flops | bytes accessed | tf_op | source)
XLA Modules:
  0.0 30.2 jit_solution(18015587987502902648)
XLA Ops:
  0.6 28.7 %shard_map.59 = (f32[4,8,16,256]{3,2,1,0:T(8,128)S(1)}, f32[4,4096]{1,0:T(4,128)S(1)}) custom-call(f32[2,4,8,16,256]{4,3,2,1,0:T(8,128)} %bitcast.4, s32[4,8,16,256]{3,2,1,0:T(8,128)} %bitcast.5, f32[3,8]{1,0:T(4,128)} %colour_source.1, f32[8]{0:T(128)} %extinction_source.1), custom_call_target="tpu_custom_call" | custom-call | tf_op jit(solution)/shard_map/pallas_call | solution.py:381
  29.4 0.8 %shard_map.60 = (f32[4,128,256]{2,1,0:T(8,128)}, f32[4,4096]{1,0:T(4,128)}) custom-call(f32[4,128,256]{2,1,0:T(8,128)S(1)} %bitcast.3, f32[4,4096]{1,0:T(4,128)S(1)} %get-tuple-element.5.image), custom_call_target="tpu_custom_call" | custom-call | tf_op jit(solution)/shard_map/pallas_call | solution.py:356

commit v2 on v1

--- a/solution.py
+++ b/solution.py
@@ -74,14 +74,32 @@
     material_sem,
     back_sem,
     piece_sem,
-    plane_sem,
-    ready_sem,
-    go_sem,
+    near_sem,
+    all_sem,
+    slab_sem,
 ):
     slabs, members, depth, rows, cols, chunk_rows, chunk_cols = dims
     slab = lax.axis_index("slab")
     me = lax.axis_index("swap")
-    gate = 1
+    head, tail = 2, members - 2
+
+    def each(low, high, skip=None):
+        def run(body):
+            def visit(m):
+                wanted = m != me
+                if skip is not None:
+                    wanted = jnp.logical_and(wanted, m != skip)
+                pl.when(wanted)(lambda: body(m))
+
+            for core in range(2):
+                if high - low <= 8:
+                    for m in range(low + core, high, 2):
+                        visit(m)
+                else:
+                    pl.loop(0, (high - low) // 2)(lambda k, core=core: visit(low + 2 * k + core))
+
+        return run
+
     layers = members * depth
     width = STEPS
     across = cols // chunk_cols
@@ -127,68 +145,111 @@
     barrier = pltpu.get_barrier_semaphore()
     behind = lax.rem(slab + slabs - 1, slabs)
     ahead = lax.rem(slab + 1, slabs)
-    def to_other_slabs(sem):
-        @pl.loop(1, slabs)
-        def _(k):
-            pl.semaphore_signal(
-                sem, inc=1, device_id=(lax.rem(slab + k, slabs), me), device_id_type=MESH
-            )
-
-    def to_plane(sem):
-        @pl.loop(1, members)
-        def _(k):
-            other = lax.rem(me + k, members)
-
-            @pl.when(other != gate)
-            def _():
-                pl.semaphore_signal(sem, inc=1, device_id=(slab, other), device_id_type=MESH)
-
-    to_plane(barrier)
-
-    @pl.when(me == gate)
-    def _():
-        to_other_slabs(barrier)
-
-    @pl.when(me != gate)
-    def _():
-        pl.semaphore_wait(barrier, members - 1)
-        pl.semaphore_signal(plane_sem, inc=1, device_id=(slab, gate), device_id_type=MESH)
-
-    @pl.when(me == gate)
-    def _():
-        pl.semaphore_wait(plane_sem, members - 1)
-
-    def send_fields(c):
-        r, l = spot(c)
-        @pl.loop(1, members)
-        def _(k):
-            other = lax.rem(me + k, members)
-            pltpu.make_async_remote_copy(
-                src_ref=staged.at[:, :, other, r, l],
-                dst_ref=held.at[c, :, mine],
-                send_sem=send_sem.at[0],
-                recv_sem=field_sem.at[c, me],
-                device_id=(slab, other),
-                device_id_type=MESH,
-            ).start()
+    early = me < head
+    late = me >= tail
+    paired = lax.rem(me, 2) == 1
+
+    def to_range(sem, low, high):
+        @pl.loop(low, high)
+        def _(m):
+            pl.semaphore_signal(sem, inc=1, device_id=(slab, m), device_id_type=MESH)
+
+    def to_slabs(sem, low, high):
+        @pl.loop(low, high)
+        def _(n):
+            pl.semaphore_signal(sem, inc=1, device_id=(n, me), device_id_type=MESH)
+
+    @pl.when(jnp.logical_not(paired))
+    def _():
+        to_range(barrier, me + 1, me + 2)
+
+    @pl.when(early)
+    def _():
+        to_range(barrier, head, members)
+
+    @pl.when(jnp.logical_and(me >= head, me < tail))
+    def _():
+        to_range(barrier, tail, members)
+
+    to_slabs(barrier, slab + 1, slabs)
+    def wait_count(sem, count):
+        @pl.when(count > 0)
+        def _():
+            pl.semaphore_wait(sem, count)
+
+    wait_count(
+        barrier,
+        jnp.where(early, 0, jnp.where(late, tail, head)) + jnp.where(paired, 1, 0) + slab,
+    )
+
+    @pl.when(paired)
+    def _():
+        to_range(near_sem, me - 1, me)
+
+    @pl.when(late)
+    def _():
+        to_range(all_sem, 0, tail)
+
+    @pl.when(jnp.logical_and(me >= head, me < tail))
+    def _():
+        to_range(near_sem, 0, head)
+
+    to_slabs(slab_sem, 0, slab)
+    wait_count(near_sem, jnp.where(early, tail - head, 0) + jnp.where(paired, 0, 1))
+
+    def field_copy(c, other):
+        r, l = spot(c)
+        return pltpu.make_async_remote_copy(
+            src_ref=staged.at[:, :, other, r, l],
+            dst_ref=held.at[c, :, mine],
+            send_sem=send_sem.at[0],
+            recv_sem=field_sem.at[c, me],
+            device_id=(slab, other),
+            device_id_type=MESH,
+        )
+
+    def send_fields(c, low, high, skip=None):
+        @each(low, high, skip)
+        def _(other):
+            field_copy(c, other).start()
 
     def send_material(c):
         r, l = spot(c)
-        @pl.loop(1, members)
-        def _(k):
-            other = lax.rem(me + k, members)
+
+        @each(0, members)
+        def _(other):
             pltpu.make_async_remote_copy(
                 src_ref=staged_material.at[:, other, r, l],
                 dst_ref=held_material.at[c, mine_material],
                 send_sem=send_sem.at[1],
-                recv_sem=material_sem.at[c],
+                recv_sem=material_sem.at[c, me],
                 device_id=(slab, other),
                 device_id_type=MESH,
             ).start()
 
-    for c in range(chunks):
+    loads[0].wait()
+
+    @pl.when(early)
+    def _():
+        send_fields(0, 0, tail)
+        pl.semaphore_wait(all_sem, members - tail)
+        send_fields(0, tail, members)
+
+    @pl.when(jnp.logical_and(me >= head, me < tail))
+    def _():
+        buddy = me + 1 - 2 * lax.rem(me, 2)
+        send_fields(0, 0, head)
+        field_copy(0, buddy).start()
+        pl.semaphore_wait(all_sem, members - tail)
+        send_fields(0, head, members, buddy)
+
+    @pl.when(late)
+    def _():
+        send_fields(0, 0, members)
+
+    for c in range(1, chunks):
         loads[c].wait()
-        send_fields(c)
+        send_fields(c, 0, members)
     for c in range(chunks):
         material_loads[c].wait()
         send_material(c)
@@ -199,19 +260,10 @@
             staged.at[:, :, me, r, l], held.at[c, :, mine], field_sem.at[c, me]
         ).start()
         pltpu.make_async_copy(
-            staged_material.at[:, me, r, l], held_material.at[c, mine_material], material_sem.at[c]
+            staged_material.at[:, me, r, l], held_material.at[c, mine_material], material_sem.at[c, me]
         ).start()
 
-    @pl.when(me == gate)
-    def _():
-        pl.semaphore_wait(barrier, slabs - 1)
-        to_other_slabs(ready_sem)
-        pl.semaphore_wait(ready_sem, slabs - 1)
-        to_plane(go_sem)
-
-    @pl.when(me != gate)
-    def _():
-        pl.semaphore_wait(go_sem, 1)
+    wait_count(slab_sem, slabs - 1 - slab)
 
     def wait_for(ref, sem):
         pltpu.make_async_copy(ref, ref, sem).wait()
@@ -246,9 +298,8 @@
 
     def send_back(c):
         r, l = spot(c)
-        @pl.loop(1, members)
-        def _(k):
-            other = lax.rem(me + k, members)
+        @each(0, members)
+        def _(other):
             pltpu.make_async_remote_copy(
                 src_ref=new_density.at[c, pl.ds(other * depth, depth)],
                 dst_ref=out_density.at[:, me, r, l],
@@ -266,13 +317,14 @@
     scale = DEPTH_SCALE / (slabs * layers)
 
     def render(c):
-        wait_for(held_material.at[c], material_sem.at[c])
         zero = jnp.zeros((chunk_rows, chunk_cols), jnp.float32)
         rates = [extinction_table[n] * (-scale) for n in range(materials)]
         colours = [[colour_table[ch, n] for n in range(materials)] for ch in range(3)]
 
         through, sums = zero + 1.0, (zero,) * 3
         for i in range(layers):
+            if i % depth == 0:
+                wait_for(held_material.at[c, pl.ds(i, depth)], material_sem.at[c, i // depth])
             row = held_material[c, i]
             masks = [(row & (1 << bit)) != 0 for bit in range((materials - 1).bit_length())]
             rate = lookup(masks, rates)
@@ -411,7 +463,7 @@
             pltpu.SemaphoreType.DMA((5,)),
             pltpu.SemaphoreType.DMA((chunks, members)),
             pltpu.SemaphoreType.DMA((chunks, 2)),
-            pltpu.SemaphoreType.DMA((chunks,)),
+            pltpu.SemaphoreType.DMA((chunks, members)),
             pltpu.SemaphoreType.DMA,
             pltpu.SemaphoreType.DMA((chunks,)),
             pltpu.SemaphoreType.REGULAR,

time: 30.7 us -> 30 us (0.977); the launches traced: 30.2 us -> 29.9 us
  no operation moved by 1% of the time
where the time goes in v2:
time: 30 us; the launch traced here: 29.9 us
  Pallas kernels  29.2 us (97%)
  between operations  0.64 us (2%)
    pallas_call x1, Pallas kernels, per_device(): pl.pallas_call(functools.partial(kernel, dims), out_shape=(pltpu.VMEM((de...  28.4 us
    pallas_call x1, Pallas kernels, write_out(): pl.pallas_call(put_kernel, out_shape=(jax.ShapeDtypeStruct(density.shape,...  0.82 us

profile of v2, /device:TPU:5, one launch (start us, length us, event | category | flops | bytes accessed | tf_op | source)
XLA Modules:
  0.0 29.9 jit_solution(14381744668858514273)
XLA Ops:
  0.6 28.4 %shard_map.59 = (f32[4,8,16,256]{3,2,1,0:T(8,128)S(1)}, f32[4,4096]{1,0:T(4,128)S(1)}) custom-call(f32[2,4,8,16,256]{4,3,2,1,0:T(8,128)} %bitcast.4, s32[4,8,16,256]{3,2,1,0:T(8,128)} %bitcast.5, f32[3,8]{1,0:T(4,128)} %colour_source.1, f32[8]{0:T(128)} %extinction_source.1), custom_call_target="tpu_custom_call" | custom-call | tf_op jit(solution)/shard_map/pallas_call | solution.py:433
  29.1 0.8 %shard_map.60 = (f32[4,128,256]{2,1,0:T(8,128)}, f32[4,4096]{1,0:T(4,128)}) custom-call(f32[4,128,256]{2,1,0:T(8,128)S(1)} %bitcast.3, f32[4,4096]{1,0:T(4,128)S(1)} %get-tuple-element.5.image), custom_call_target="tpu_custom_call" | custom-call | tf_op jit(solution)/shard_map/pallas_call | solution.py:408

commit v3 on v2

--- a/solution.py
+++ b/solution.py
@@ -61,6 +61,7 @@
     held_material,
     new_density,
     pieces,
+    rest,
     image,
     colour_table,
     extinction_table,
@@ -133,7 +134,6 @@
                 load_material_sem.at[c],
             )
         )
-        material_loads[-1].start()
 
     tables = (
         pltpu.make_async_copy(colour_source, colour_table, table_sem.at[0]),
@@ -228,6 +228,8 @@
             ).start()
 
     loads[0].wait()
+    for load in material_loads:
+        load.start()
 
     @pl.when(early)
     def _():
@@ -285,9 +287,11 @@
 
     total = layers + 2 * width
 
-    def sweep(c):
+    front = -(-width // depth)
+
+    def stream(c, start, stop):
         states = [None] * STEPS
-        for i in range(total):
+        for i in range(start, stop):
             cell = held[c, 0, i], held[c, 1, i]
             for k in range(STEPS):
                 states[k], cell = advance(states[k], *cell)
@@ -297,9 +301,10 @@
                 new_density[c, i - 2 * width] = cell[0]
 
     def send_back(c):
-        r, l = spot(c)
-        @each(0, members)
-        def _(other):
+        r = pl.ds(pl.multiple_of(c // across * chunk_rows, chunk_rows), chunk_rows)
+        l = pl.ds(pl.multiple_of(c % across * chunk_cols, chunk_cols), chunk_cols)
+
+        def send(other):
             pltpu.make_async_remote_copy(
                 src_ref=new_density.at[c, pl.ds(other * depth, depth)],
                 dst_ref=out_density.at[:, me, r, l],
@@ -308,21 +313,31 @@
                 device_id=(slab, other),
                 device_id_type=MESH,
             ).start()
+
+        each(0, members)(send)
         pltpu.make_async_copy(
-            new_density.at[c, pl.ds(me * depth, depth)],
-            out_density.at[:, me, r, l],
-            back_sem,
+            new_density.at[c, pl.ds(me * depth, depth)], out_density.at[:, me, r, l], back_sem
         ).start()
 
+    def sweep_rest(c):
+        for m in range(1, members - 1):
+            wait_for(held.at[c, :, pl.ds(width + m * depth, depth)], field_sem.at[c, m])
+        wait_for(held.at[c, :, pl.ds(0, width)], halo_sem.at[c, 1])
+        stream(c, width, total)
+
+    def sweep_front(c):
+        wait_for(held.at[c, :, pl.ds(0, width)], halo_sem.at[c, 0])
+        stream(c, 0, 3 * width)
+        send_back(c)
+
     scale = DEPTH_SCALE / (slabs * layers)
 
-    def render(c):
+    def absorb(c, low, high):
         zero = jnp.zeros((chunk_rows, chunk_cols), jnp.float32)
         rates = [extinction_table[n] * (-scale) for n in range(materials)]
         colours = [[colour_table[ch, n] for n in range(materials)] for ch in range(3)]
-
         through, sums = zero + 1.0, (zero,) * 3
-        for i in range(layers):
+        for i in range(low * depth, high * depth):
             if i % depth == 0:
                 wait_for(held_material.at[c, pl.ds(i, depth)], material_sem.at[c, i // depth])
             row = held_material[c, i]
@@ -332,9 +347,19 @@
             weight = through * (1.0 - kept)
             sums = tuple(s + weight * lookup(masks, t) for s, t in zip(sums, colours))
             through = through * kept
+        return sums, through
+
+    def render_rest(c):
+        sums, through = absorb(c, front, members)
         for ch in range(3):
-            pieces[c, slab, ch] = sums[ch]
-        pieces[c, slab, 3] = through
+            rest[ch] = sums[ch]
+        rest[3] = through
+
+    def render_front(c):
+        sums, through = absorb(c, 0, front)
+        for ch in range(3):
+            pieces[c, slab, ch] = sums[ch] + through * rest[ch]
+        pieces[c, slab, 3] = through * rest[3]
 
         @pl.loop(1, slabs)
         def _(k):
@@ -351,24 +376,27 @@
     for table in tables:
         table.wait()
 
-    @pl.loop(0, chunks)
+    end = chunks - 1
+
+    @pl.loop(0, end)
     def _(c):
-        @pl.when(c + 1 < chunks)
-        def _():
-            pass_halos(c + 1)
-
-        for m in range(1, members - 1):
-            wait_for(held.at[c, :, pl.ds(width + m * depth, depth)], field_sem.at[c, m])
-        for side in range(2):
-            wait_for(held.at[c, :, pl.ds(0, width)], halo_sem.at[c, side])
-        sweep(c)
-        send_back(c)
+        pass_halos(c + 1)
+        sweep_rest(c)
+        sweep_front(c)
 
         @pl.when(c > 0)
         def _():
-            render(c - 1)
-
-    render(chunks - 1)
+            render_rest(c - 1)
+            render_front(c - 1)
+
+    sweep_rest(end)
+    if end > 0:
+        render_rest(end - 1)
+        render_front(end - 1)
+    sweep_front(end)
+    render_rest(end)
+    render_front(end)
+
     for c in range(chunks):
         wait_for(pieces.at[c, pl.ds(0, slabs - 1)], piece_sem.at[c])
         through = pieces[c, 0, 3]
@@ -453,6 +481,7 @@
             pltpu.VMEM((chunks, layers) + tile, jnp.int32),
             pltpu.VMEM((chunks, layers) + tile, jnp.float32),
             pltpu.VMEM((chunks, slabs, 4) + tile, jnp.float32),
+            pltpu.VMEM((4,) + tile, jnp.float32),
             pltpu.VMEM((4, rows * cols), jnp.float32),
             pltpu.SMEM(table_colour.shape, jnp.float32),
             pltpu.SMEM(table_extinction.shape, jnp.float32),

time: 30 us -> 29.7 us (0.990)
  Pallas kernels: 29.2 us -> 28.9 us
    pallas_call x1, Pallas kernels: 28.4 us -> 28 us  [per_device(): pl.pallas_call(functools.partial(kernel, dims), out_shape=(pltpu.VMEM((de...]
where the time goes in v3:
time: 29.7 us; the launch traced here: 29.5 us
  Pallas kernels  28.9 us (97%)
  between operations  0.64 us (2%)
    pallas_call x1, Pallas kernels, per_device(): pl.pallas_call(functools.partial(kernel, dims), out_shape=(pltpu.VMEM((de...  28 us
    pallas_call x1, Pallas kernels, write_out(): pl.pallas_call(put_kernel, out_shape=(jax.ShapeDtypeStruct(density.shape,...  0.82 us

profile of v3, /device:TPU:5, one launch (start us, length us, event | category | flops | bytes accessed | tf_op | source)
XLA Modules:
  0.0 29.5 jit_solution(14352181313220402795)
XLA Ops:
  0.6 28.0 %shard_map.59 = (f32[4,8,16,256]{3,2,1,0:T(8,128)S(1)}, f32[4,4096]{1,0:T(4,128)S(1)}) custom-call(f32[2,4,8,16,256]{4,3,2,1,0:T(8,128)} %bitcast.4, s32[4,8,16,256]{3,2,1,0:T(8,128)} %bitcast.5, f32[3,8]{1,0:T(4,128)} %colour_source.1, f32[8]{0:T(128)} %extinction_source.1), custom_call_target="tpu_custom_call" | custom-call | tf_op jit(solution)/shard_map/pallas_call | solution.py:461
  28.7 0.8 %shard_map.60 = (f32[4,128,256]{2,1,0:T(8,128)}, f32[4,4096]{1,0:T(4,128)}) custom-call(f32[4,128,256]{2,1,0:T(8,128)S(1)} %bitcast.3, f32[4,4096]{1,0:T(4,128)S(1)} %get-tuple-element.5.image), custom_call_target="tpu_custom_call" | custom-call | tf_op jit(solution)/shard_map/pallas_call | solution.py:436
